TPU v7x, 32 devices: a whole 2x2x4 slice. The times are simulated.
32 devices in a mesh: seq: 4 (over y, x), tp: 8 (over z, core).
Axes of the slice: x: 2, y: 2, z: 4, core: 2. Of those that a mesh axis runs over, the one named last changes fastest.
Arguments:
- tokens: bfloat16 [1, 512, 4096], P(None, 'seq', 'tp'), may hold values from -6 to 6
- projections: bfloat16 [4096, 3, 4096], P(None, None, 'tp'), may hold values from -1.5 to 1.5
- out_weight: bfloat16 [4096, 4096], P('tp'), may hold values from -0.09375 to 0.09375
- gain_in: float32 [4096], P('tp'), may hold values from 0.5 to 1.5
- gain_out: float32 [4096], P('tp'), may hold values from 0.5 to 1.5
- iterates: float32 [5, 1, 512, 4096], P(None, None, 'seq', 'tp'), may hold values from -5 to 5
- images: float32 [5, 1, 512, 4096], P(None, None, 'seq', 'tp'), may hold values from -330 to 330
Outputs:
- mixed: float32 [1, 512, 4096], P(None, 'seq', 'tp')
- image: float32 [1, 512, 4096], P(None, 'seq', 'tp')
All inputs are finite; a program needn't handle non-finite values.
Results may differ from a plain program's by a relative error of at most 0.013.
Values may be sent and summed in bfloat16 or wider, within the bound.
A program may use at most 64 MiB of HBM per device.

v0:
```python
import functools

import jax
import jax.numpy as jnp
import numpy as np
from jax import lax
from jax.experimental import pallas as pl
from jax.experimental.pallas import tpu as pltpu
from jax.sharding import PartitionSpec as P

HEAD_SIZE = 128
ITERS = 2
MESH = pl.DeviceIdType.MESH

epsilon = 1e-05
rope_base = 10000.0
ridge_factor = 0.01

f32 = jnp.float32
bf16 = jnp.bfloat16


def rope_tables(length):
    half = HEAD_SIZE // 2
    frequency = rope_base ** (-2.0 * np.arange(half) / HEAD_SIZE)
    angles = np.arange(length)[:, None] * frequency[None, :]
    cosine, sine = np.cos(angles), np.sin(angles)
    return np.stack(
        [np.concatenate([cosine, cosine], 1), np.concatenate([-sine, sine], 1)]
    ).astype(np.float32)


def anderson_weights(gram):
    extent = len(gram)
    trace = gram[0][0]
    for m in range(1, extent):
        trace = trace + gram[m][m]
    ridge = ridge_factor * trace / extent
    matrix = [[gram[m][n] + ridge if m == n else gram[m][n] for n in range(extent)] for m in range(extent)]
    target = [jnp.ones_like(ridge) for _ in range(extent)]
    for column in range(extent):
        for row in range(column + 1, extent):
            factor = matrix[row][column] / matrix[column][column]
            for k in range(column + 1, extent):
                matrix[row][k] = matrix[row][k] - factor * matrix[column][k]
            target[row] = target[row] - factor * target[column]
    answer = [None] * extent
    for column in reversed(range(extent)):
        value = target[column]
        for k in range(column + 1, extent):
            value = value - matrix[column][k] * answer[k]
        answer[column] = value / matrix[column][column]
    total = answer[0]
    for m in range(1, extent):
        total = total + answer[m]
    return [a / total for a in answer]


def kernel(
    n_seq, n_tp,
    tokens, proj_hbm, out_hbm, gain_in, gain_out, iterates, images, rope_hbm,
    mixed_out, image_out,
    proj, out_w, rope, xbuf, acc, kv, qbuf, att, psend, precv, zsend, zrecv,
    summed, colbuf, tp_stat, seq_stat,
    load_sem, tp_send, tp_recv, seq_send, seq_recv, x_send, x_recv, r_send, r_recv,
    kv_send, kv_recv, p_send, p_recv, z_send, z_recv,
):
    mem, length, width = images.shape
    heads = qbuf.shape[1] // HEAD_SIZE
    embed = qbuf.shape[1]
    n_z = n_tp // 2
    full_width = n_tp * width
    seq = lax.axis_index("seq")
    tp = lax.axis_index("tp")
    core = lax.rem(tp, 2)
    z = lax.div(tp, 2)
    partner = z * 2 + 1 - core
    CH = 16
    chunks = length // CH
    lane = lax.broadcasted_iota(jnp.int32, (CH, 128), 1)
    pending = []

    loads = [
        pltpu.make_async_copy(proj_hbm, proj, load_sem.at[0]),
        pltpu.make_async_copy(out_hbm, out_w, load_sem.at[1]),
        pltpu.make_async_copy(
            rope_hbm.at[:, pl.ds(pl.multiple_of(seq * length, 128), length), :], rope, load_sem.at[2]
        ),
    ]
    for load in loads:
        load.start()

    barrier = pltpu.get_barrier_semaphore()
    for d in range(1, n_tp):
        pl.semaphore_signal(barrier, inc=1, device_id={"tp": lax.rem(tp + d, n_tp)}, device_id_type=MESH)
    for d in range(1, n_seq):
        pl.semaphore_signal(barrier, inc=1, device_id={"seq": lax.rem(seq + d, n_seq)}, device_id_type=MESH)

    def remote(src, dst, send, recv, device):
        return pltpu.make_async_remote_copy(
            src_ref=src, dst_ref=dst, send_sem=send, recv_sem=recv, device_id=device, device_id_type=MESH
        )

    def post(buf, sends, recvs, phase, axis, me, n, count):
        copies = []
        rows = pl.ds(0, count)
        for d in range(1, n):
            copy = remote(
                buf.at[phase, me, rows], buf.at[phase, me, rows], sends.at[phase, d], recvs.at[phase, d],
                {axis: lax.rem(me + d, n)},
            )
            copy.start()
            copies.append(copy)
        pending.extend(copies)
        return copies

    def collect(buf, copies, phase, n, count=16):
        for copy in copies:
            copy.wait_recv()
        total = buf[phase, 0, :count]
        for j in range(1, n):
            total = total + buf[phase, j, :count]
        return total

    def post_tp(phase, count=16):
        return post(tp_stat, tp_send, tp_recv, phase, "tp", tp, n_tp, count)

    def post_seq(phase, count=16):
        return post(seq_stat, seq_send, seq_recv, phase, "seq", seq, n_seq, count)

    pairs = [(m, n) for m in range(mem) for n in range(m, mem)]

    def gram_step(i, sums):
        rows = pl.ds(pl.multiple_of(i * 8, 8), 8)
        res = [images[m, rows, :] - iterates[m, rows, :] for m in range(mem)]
        out = []
        for (m, n), total in zip(pairs, sums):
            product = res[m] * res[n]
            for c in range(width // 128):
                total = total + product[:, c * 128:(c + 1) * 128]
            out.append(total)
        return tuple(out)

    sums = lax.fori_loop(0, length // 8, gram_step, tuple(jnp.zeros((8, 128), f32) for _ in pairs))
    for p, total in enumerate(sums):
        tp_stat[0, tp, pl.ds(p, 1), :] = jnp.sum(total, axis=0, keepdims=True)
    tp_stat[0, tp, pl.ds(len(pairs), 1), :] = jnp.zeros((1, 128), f32)

    for it in range(ITERS):
        for j in range(1, n_seq):
            @pl.when(j > seq)
            def _():
                kv[it, :, j, 1] = jnp.zeros((heads, length, HEAD_SIZE), bf16)

    pl.semaphore_wait(barrier, n_tp - 1 + n_seq - 1)

    stage = collect(tp_stat, post_tp(0), 0, n_tp)
    seq_stat[0, seq] = stage
    entries = collect(seq_stat, post_seq(0), 0, n_seq)

    def spread(rows):
        return jnp.broadcast_to(jnp.sum(rows, axis=1, keepdims=True), rows.shape)

    entries = spread(entries)
    gram = [[None] * mem for _ in range(mem)]
    for p, (m, n) in enumerate(pairs):
        gram[m][n] = gram[n][m] = entries[p:p + 1, :]

    halves = xbuf.shape[2]
    part = width // halves
    steps = (1, -1)

    def inside(place):
        return jnp.logical_and(place >= 0, place < n_z)

    def guarded(condition, act):
        @pl.when(condition)
        def _():
            act()

    for it in range(ITERS):
        last = it + 1 == ITERS
        alpha = [a[:, :1] for a in anderson_weights(gram)]

        def mix_step(i, carry):
            rows = pl.ds(pl.multiple_of(i * CH, CH), CH)
            stored = [images[m, rows, :] for m in range(it, mem)] + ([image_out[rows, :]] if it else [])
            mixed = alpha[0] * stored[0]
            for m in range(1, mem):
                mixed = mixed + alpha[m] * stored[m]
            mixed_out[rows, :] = mixed
            ready = (mixed * gain_in[...]).astype(bf16)
            for q in range(halves):
                xbuf[it, tp, q, rows, :] = ready[:, q * part:(q + 1) * part]
            colbuf[rows, :] = jnp.broadcast_to(jnp.sum(mixed * mixed, axis=1, keepdims=True), (CH, 128))
            return carry

        lax.fori_loop(0, chunks, mix_step, 0)

        def x_copy(side, k, q):
            slot = (z - steps[side] * (k - 1)) * 2 + core
            return remote(
                xbuf.at[it, slot, q], xbuf.at[it, slot, q], x_send.at[it, side, k, q], x_recv.at[it, side, k, q],
                {"tp": (z + steps[side]) * 2 + core},
            )

        def x_arrival(side, k, q):
            slot = (z - steps[side] * k) * 2 + core
            return remote(
                xbuf.at[it, slot, q], xbuf.at[it, slot, q], x_send.at[it, side, k, q], x_recv.at[it, side, k, q],
                {"tp": partner},
            )

        def relay(side, k, q):
            slot = (z - steps[side] * k) * 2 + core
            return remote(
                xbuf.at[it, slot, q], xbuf.at[it, slot, q], r_send.at[it, side, k, q], r_recv.at[it, side, k, q],
                {"tp": partner},
            )

        def project(slot, q):
            rows = pl.ds(pl.multiple_of(slot * width + q * part, 128), part)
            for c in range(3):
                acc[c] += jnp.dot(xbuf[it, slot, q], proj[c, rows, :], preferred_element_type=f32)

        for q in range(halves):
            for side in range(2):
                guarded(inside(z + steps[side]), x_copy(side, 1, q).start)
        for q in range(halves):
            relay(0, 0, q).start()
        tp_stat[1 + 2 * it, tp] = jnp.transpose(colbuf[...])[:16, :]
        square_copies = post_tp(1 + 2 * it, 1)
        if it == 0:
            loads[0].wait()
        acc[...] = jnp.zeros(acc.shape, f32)
        for q in range(halves):
            project(tp, q)
        for q in range(halves):
            relay(0, 0, q).wait_recv()
            project(partner, q)

        def arrive(side, k, q):
            x_arrival(side, k, q).wait_recv()
            if k + 1 < n_z:
                guarded(inside(z + steps[side]), x_copy(side, k + 1, q).start)
            relay(side, k, q).start()

        def across(side, k, q):
            relay(side, k, q).wait_recv()
            project((z - steps[side] * k) * 2 + 1 - core, q)

        for k in range(1, n_z):
            for q in range(halves):
                for side in range(2):
                    guarded(inside(z - steps[side] * k), functools.partial(arrive, side, k, q))
                for side in range(2):
                    guarded(
                        inside(z - steps[side] * k),
                        functools.partial(project, (z - steps[side] * k) * 2 + core, q),
                    )
                for side in range(2):
                    guarded(inside(z - steps[side] * k), functools.partial(across, side, k, q))
        squares = collect(tp_stat, square_copies, 1 + 2 * it, n_tp, 1)
        row_scale = jnp.transpose(
            jnp.broadcast_to(lax.rsqrt(squares / full_width + epsilon), (length, length))
        )
        if it == 0:
            loads[2].wait()
        cosine, sine = rope[0] * row_scale, rope[1] * row_scale

        def rotated(c, cols):
            rows = acc[c, :, cols]
            return (rows * cosine + pltpu.roll(rows, HEAD_SIZE // 2, 1) * sine).astype(bf16)

        kv_copies = [[] for _ in range(heads)]
        for h in range(heads):
            cols = slice(h * HEAD_SIZE, (h + 1) * HEAD_SIZE)
            kv[it, h, seq, 0] = rotated(1, cols)
            kv[it, h, seq, 1] = (acc[2, :, cols] * row_scale).astype(bf16)
            for d in reversed(range(1, n_seq)):
                copy = remote(
                    kv.at[it, h, seq], kv.at[it, h, seq], kv_send.at[it, h, d], kv_recv.at[it, h, d],
                    {"seq": lax.rem(seq + d, n_seq)},
                )
                guarded(seq + d < n_seq, copy.start)
                kv_copies[h].append((d, copy))
        for h in range(heads):
            cols = slice(h * HEAD_SIZE, (h + 1) * HEAD_SIZE)
            qbuf[:, cols] = rotated(0, cols)

        total_keys = n_seq * length
        query_index = seq * length + lax.broadcasted_iota(jnp.int32, (length, total_keys), 0)
        allowed = lax.broadcasted_iota(jnp.int32, (length, total_keys), 1) <= query_index
        for h in range(heads):
            cols = slice(h * HEAD_SIZE, (h + 1) * HEAD_SIZE)
            for d, copy in kv_copies[h]:
                guarded(seq >= d, copy.wait_recv)
            keys = kv[it, h, :, 0].reshape(total_keys, HEAD_SIZE)
            values = kv[it, h, :, 1].reshape(total_keys, HEAD_SIZE)
            scores = lax.dot_general(
                qbuf[:, cols], keys, (((1,), (1,)), ((), ())), preferred_element_type=f32
            ) * HEAD_SIZE ** (-0.5)
            scores = jnp.where(allowed, scores, -1e30)
            weights = jnp.where(allowed, jnp.exp(scores - jnp.max(scores, axis=1, keepdims=True)), 0.0)
            total = jnp.sum(weights, axis=1, keepdims=True)
            mixture = jnp.dot(weights.astype(bf16), values, preferred_element_type=f32)
            att[:, cols] = (mixture / total).astype(bf16)

        if it == 0:
            loads[1].wait()

        def partial(place, side_core, q):
            cols = pl.ds(pl.multiple_of((place * 2 + side_core) * width + q * part, 128), part)
            return jnp.dot(att[...], out_w[:, cols], preferred_element_type=f32)

        def p_copy(side, k, q):
            return remote(
                psend.at[it, side, k, q], precv.at[it, side, k, q],
                p_send.at[it, side, k, q], p_recv.at[it, side, k, q], {"tp": partner},
            )

        def z_copy(side, k, q):
            return remote(
                zsend.at[it, side, k, q], zrecv.at[it, side, k - 1, q],
                z_send.at[it, side, k, q], z_recv.at[it, side, k - 1, q],
                {"tp": (z + steps[side]) * 2 + core},
            )

        def arrival(side, k, q):
            return remote(
                zsend.at[it, side, k, q], zrecv.at[it, side, k, q],
                z_send.at[it, side, k, q], z_recv.at[it, side, k, q],
                {"tp": partner},
            )

        def give(side, k, q):
            psend[it, side, k, q] = partial(z + steps[side] * k, 1 - core, q).astype(bf16)
            p_copy(side, k, q).start()

        def pass_on(side, k, q):
            own = partial(z + steps[side] * k, core, q)
            p_copy(side, k, q).wait_recv()
            own = own + precv[it, side, k, q].astype(f32)
            if k + 1 < n_z:
                behind = inside(z - steps[side])
                guarded(behind, arrival(side, k, q).wait_recv)
                own = own + jnp.where(behind, zrecv[it, side, k, q].astype(f32), 0.0)
            zsend[it, side, k, q] = own.astype(bf16)
            z_copy(side, k, q).start()

        for k in reversed(range(1, n_z)):
            for q in range(halves):
                for side in range(2):
                    guarded(inside(z + steps[side] * k), functools.partial(give, side, k, q))
        for q in range(halves):
            give(0, 0, q)
        for k in reversed(range(1, n_z)):
            for q in range(halves):
                for side in range(2):
                    guarded(inside(z + steps[side] * k), functools.partial(pass_on, side, k, q))
        for q in range(halves):
            cols = slice(q * part, (q + 1) * part)
            own = partial(z, core, q) + tokens[:, cols].astype(f32)
            p_copy(0, 0, q).wait_recv()
            summed[:, cols] = own + precv[it, 0, 0, q].astype(f32)
        for q in range(halves):
            cols = slice(q * part, (q + 1) * part)
            for side in range(2):
                def take(side=side, q=q, cols=cols):
                    arrival(side, 0, q).wait_recv()
                    summed[:, cols] += zrecv[it, side, 0, q].astype(f32)

                guarded(inside(z - steps[side]), take)

        def sum_step(i, carry):
            rows = pl.ds(pl.multiple_of(i * CH, CH), CH)
            layer = summed[rows, :]
            scaled = layer * gain_out[...]
            summed[rows, :] = scaled
            stats = [layer * layer]
            if not last:
                mixed = mixed_out[rows, :]
                kept = [images[m, rows, :] - iterates[m, rows, :] for m in range(1, mem)]
                stats += [scaled * k for k in kept] + [mixed * k for k in kept]
                stats += [scaled * scaled, scaled * mixed, mixed * mixed]
            columns = jnp.zeros((CH, 128), f32)
            for k, stat in enumerate(stats):
                columns = jnp.where(lane == k, jnp.sum(stat, axis=1, keepdims=True), columns)
            colbuf[rows, :] = columns
            return carry

        lax.fori_loop(0, chunks, sum_step, 0)
        tp_stat[2 + 2 * it, tp] = jnp.transpose(colbuf[...])[:16, :]
        count = 1 if last else 16
        stats = collect(tp_stat, post_tp(2 + 2 * it, count), 2 + 2 * it, n_tp, count)
        scale_row = lax.rsqrt(stats[:1, :] / full_width + epsilon)

        if not last:
            k = mem - 1
            for m in range(k):
                seq_stat[1, seq, pl.ds(m, 1), :] = (
                    scale_row * stats[1 + m:2 + m, :] - stats[1 + k + m:2 + k + m, :]
                )
            own = 1 + 2 * k
            seq_stat[1, seq, pl.ds(k, 1), :] = (
                scale_row * scale_row * stats[own:own + 1, :]
                - 2.0 * scale_row * stats[own + 1:own + 2, :]
                + stats[own + 2:own + 3, :]
            )
            seq_stat[1, seq, pl.ds(mem, 16 - mem), :] = jnp.zeros((16 - mem, 128), f32)
            seq_copies = post_seq(1)
        scale_cols = jnp.transpose(jnp.broadcast_to(scale_row, (length, length)))
        for c in range(width // 128):
            cols = slice(c * 128, (c + 1) * 128)
            image_out[:, cols] = summed[:, cols] * scale_cols
        if not last:
            new = spread(collect(seq_stat, seq_copies, 1, n_seq))
            grown = [[None] * mem for _ in range(mem)]
            for m in range(mem - 1):
                for n in range(mem - 1):
                    grown[m][n] = gram[m + 1][n + 1]
                grown[m][mem - 1] = grown[mem - 1][m] = new[m:m + 1, :]
            grown[mem - 1][mem - 1] = new[mem - 1:mem, :]
            gram = grown

        for h in range(heads):
            for d, copy in kv_copies[h]:
                guarded(seq + d < n_seq, copy.wait_send)
        for q in range(halves):
            relay(0, 0, q).wait_send()
            p_copy(0, 0, q).wait_send()
            for side in range(2):
                for k in range(1, n_z):
                    guarded(
                        jnp.logical_and(inside(z + steps[side]), inside(z - steps[side] * (k - 1))),
                        x_copy(side, k, q).wait_send,
                    )
                    guarded(inside(z - steps[side] * k), relay(side, k, q).wait_send)
                    guarded(inside(z + steps[side] * k), p_copy(side, k, q).wait_send)
                    guarded(inside(z + steps[side] * k), z_copy(side, k, q).wait_send)

    for copy in pending:
        copy.wait_send()


def solution(mesh):
    n_seq, n_tp = mesh.shape["seq"], mesh.shape["tp"]

    def shards(tokens, projections, out_weight, gain_in, gain_out, iterates, images):
        batch, length, width = tokens.shape
        mem = images.shape[0]
        embed = projections.shape[2]
        n_z = n_tp // 2
        heads = embed // HEAD_SIZE
        halves = 2 if width % 256 == 0 else 1
        part = width // halves
        vmem = pl.BlockSpec(memory_space=pltpu.VMEM)
        hbm = pl.BlockSpec(memory_space=pl.ANY)
        dma = pltpu.SemaphoreType.DMA
        out = jax.ShapeDtypeStruct((length, width), f32)
        mixed, image = pl.pallas_call(
            functools.partial(kernel, n_seq, n_tp),
            out_shape=(out, out),
            in_specs=[vmem, hbm, hbm, vmem, vmem, vmem, vmem, hbm],
            out_specs=(vmem, vmem),
            scratch_shapes=[
                pltpu.VMEM((3, n_tp * width, embed), bf16),
                pltpu.VMEM((embed, n_tp * width), bf16),
                pltpu.VMEM((2, length, HEAD_SIZE), f32),
                pltpu.VMEM((ITERS, n_tp, halves, length, part), bf16),
                pltpu.VMEM((3, length, embed), f32),
                pltpu.VMEM((ITERS, heads, n_seq, 2, length, HEAD_SIZE), bf16),
                pltpu.VMEM((length, embed), bf16),
                pltpu.VMEM((length, embed), bf16),
                pltpu.VMEM((ITERS, 2, n_z, halves, length, part), bf16),
                pltpu.VMEM((ITERS, 2, n_z, halves, length, part), bf16),
                pltpu.VMEM((ITERS, 2, n_z, halves, length, part), bf16),
                pltpu.VMEM((ITERS, 2, n_z, halves, length, part), bf16),
                pltpu.VMEM((length, width), f32),
                pltpu.VMEM((length, 128), f32),
                pltpu.VMEM((1 + 2 * ITERS, n_tp, 16, 128), f32),
                pltpu.VMEM((ITERS, n_seq, 16, 128), f32),
                dma((3,)),
                dma((1 + 2 * ITERS, n_tp)), dma((1 + 2 * ITERS, n_tp)),
                dma((ITERS, n_seq)), dma((ITERS, n_seq)),
                dma((ITERS, 2, n_z, halves)), dma((ITERS, 2, n_z, halves)),
                dma((ITERS, 2, n_z, halves)), dma((ITERS, 2, n_z, halves)),
                dma((ITERS, heads, n_seq)), dma((ITERS, heads, n_seq)),
                dma((ITERS, 2, n_z, halves)), dma((ITERS, 2, n_z, halves)),
                dma((ITERS, 2, n_z, halves)), dma((ITERS, 2, n_z, halves)),
            ],
            compiler_params=pltpu.CompilerParams(
                collective_id=0, has_side_effects=True, vmem_limit_bytes=60 * 1024 * 1024
            ),
            name="anderson_layer",
        )(
            tokens.reshape(length, width),
            projections.transpose(1, 0, 2),
            out_weight,
            gain_in.reshape(1, width),
            gain_out.reshape(1, width),
            iterates.reshape(mem, length, width),
            images.reshape(mem, length, width),
            jnp.asarray(rope_tables(n_seq * length)),
        )
        return mixed.reshape(batch, length, width), image.reshape(batch, length, width)

    in_specs = (
        P(None, "seq", "tp"),
        P(None, None, "tp"),
        P("tp", None),
        P("tp"),
        P("tp"),
        P(None, None, "seq", "tp"),
        P(None, None, "seq", "tp"),
    )
    out_specs = (P(None, "seq", "tp"), P(None, "seq", "tp"))
    return jax.shard_map(shards, mesh=mesh, in_specs=in_specs, out_specs=out_specs, check_vma=False)
```

profile of v0, /device:TPU:2, one launch (start us, length us, event | category | flops | bytes accessed | tf_op | source)
XLA Modules:
  0.0 117.1 jit_solution(14316176132542273074)
XLA Ops:
  0.6 113.1 %anderson_layer.1 = (f32[128,512]{1,0:T(8,128)}, f32[128,512]{1,0:T(8,128)}) custom-call(bf16[128,512]{1,0:T(8,128)(2,1)} %bitcast.13, bf16[3,4096,512]{2,1,0:T(8,128)(2,1)} %bitcast.8, bf16[512,4096]{1,0:T(8,128)(2,1)} %out_hbm.1, f32[1,512]{1,0:T(1,128)} %bitcast.14, f32[1,512]{1,0:T(1,128)} %bitcast.15, f32[5,128,512]{2,1,0:T(8,128)} %bitcast.9, ...), custom_call_target="tpu_custom_call" | custom-call | tf_op jit(solution)/shard_map/anderson_layer/pallas_call | solution.py:461
  113.7 1.7 %copy.12 = f32[1,128,512]{2,1,0:T(8,128)} copy(f32[1,128,512]{2,1,0:T(8,128)} %bitcast.12) | data formatting | bytes 524288
  115.4 1.7 %copy.13 = f32[1,128,512]{2,1,0:T(8,128)} copy(f32[1,128,512]{2,1,0:T(8,128)} %bitcast.11) | data formatting | bytes 524288
where the time goes:
time: 117 us
  Pallas kernels  113 us (97%)
  local copies, waits for them, and re-layouts  3.34 us (3%)
    pallas_call x1, Pallas kernels, shards(): pl.pallas_call(functools.partial(kernel, n_seq, n_tp), out_shape=(out, ou...  113 us
    unnamed x2, local copies, waits for them, and re-layouts  3.34 us

commit v1 on v0

--- a/solution.py
+++ b/solution.py
@@ -15,6 +15,8 @@
 epsilon = 1e-05
 rope_base = 10000.0
 ridge_factor = 0.01
+
+LANES = 128
 
 f32 = jnp.float32
 bf16 = jnp.bfloat16
@@ -56,18 +58,23 @@
     return [a / total for a in answer]
 
 
+def swaps_heads(n_seq, heads):
+    return heads % n_seq == 0 and n_seq & (n_seq - 1) == 0
+
+
 def kernel(
     n_seq, n_tp,
     tokens, proj_hbm, out_hbm, gain_in, gain_out, iterates, images, rope_hbm,
     mixed_out, image_out,
     proj, out_w, rope, xbuf, acc, kv, qbuf, att, psend, precv, zsend, zrecv,
-    summed, colbuf, tp_stat, seq_stat,
+    summed, colbuf, tp_stat, seq_stat, stage, piece,
     load_sem, tp_send, tp_recv, seq_send, seq_recv, x_send, x_recv, r_send, r_recv,
-    kv_send, kv_recv, p_send, p_recv, z_send, z_recv,
+    kv_send, kv_recv, p_send, p_recv, z_send, z_recv, o_send, o_recv,
 ):
     mem, length, width = images.shape
-    heads = qbuf.shape[1] // HEAD_SIZE
-    embed = qbuf.shape[1]
+    embed = acc.shape[2]
+    heads = embed // HEAD_SIZE
+    swap = swaps_heads(n_seq, heads)
     n_z = n_tp // 2
     full_width = n_tp * width
     seq = lax.axis_index("seq")
@@ -114,7 +121,7 @@
         pending.extend(copies)
         return copies
 
-    def collect(buf, copies, phase, n, count=16):
+    def collect(buf, copies, phase, n, count=1):
         for copy in copies:
             copy.wait_recv()
         total = buf[phase, 0, :count]
@@ -122,10 +129,10 @@
             total = total + buf[phase, j, :count]
         return total
 
-    def post_tp(phase, count=16):
+    def post_tp(phase, count=1):
         return post(tp_stat, tp_send, tp_recv, phase, "tp", tp, n_tp, count)
 
-    def post_seq(phase, count=16):
+    def post_seq(phase, count=1):
         return post(seq_stat, seq_send, seq_recv, phase, "seq", seq, n_seq, count)
 
     pairs = [(m, n) for m in range(mem) for n in range(m, mem)]
@@ -142,26 +149,28 @@
         return tuple(out)
 
     sums = lax.fori_loop(0, length // 8, gram_step, tuple(jnp.zeros((8, 128), f32) for _ in pairs))
-    for p, total in enumerate(sums):
-        tp_stat[0, tp, pl.ds(p, 1), :] = jnp.sum(total, axis=0, keepdims=True)
-    tp_stat[0, tp, pl.ds(len(pairs), 1), :] = jnp.zeros((1, 128), f32)
-
-    for it in range(ITERS):
-        for j in range(1, n_seq):
-            @pl.when(j > seq)
-            def _():
-                kv[it, :, j, 1] = jnp.zeros((heads, length, HEAD_SIZE), bf16)
+    def packed(totals):
+        rows = [jnp.sum(total, axis=0, keepdims=True) for total in totals]
+        block = jnp.concatenate(rows + [jnp.zeros((LANES - len(rows), LANES), f32)], axis=0)
+        return jnp.sum(jnp.transpose(block), axis=0, keepdims=True)
+
+    def unpacked(row):
+        return jnp.transpose(jnp.broadcast_to(row, (LANES, LANES)))
+
+    tp_stat[0, tp, :1] = packed(sums)
+
+    if not swap:
+        for it in range(ITERS):
+            for j in range(1, n_seq):
+                @pl.when(j > seq)
+                def _():
+                    kv[it, :, j, 1] = jnp.zeros((heads, length, HEAD_SIZE), bf16)
 
     pl.semaphore_wait(barrier, n_tp - 1 + n_seq - 1)
 
-    stage = collect(tp_stat, post_tp(0), 0, n_tp)
-    seq_stat[0, seq] = stage
-    entries = collect(seq_stat, post_seq(0), 0, n_seq)
-
-    def spread(rows):
-        return jnp.broadcast_to(jnp.sum(rows, axis=1, keepdims=True), rows.shape)
-
-    entries = spread(entries)
+    seq_stat[0, seq, :1] = collect(tp_stat, post_tp(0), 0, n_tp)
+    entries = unpacked(collect(seq_stat, post_seq(0), 0, n_seq))
+
     gram = [[None] * mem for _ in range(mem)]
     for p, (m, n) in enumerate(pairs):
         gram[m][n] = gram[n][m] = entries[p:p + 1, :]
@@ -178,24 +187,101 @@
         def _():
             act()
 
+    share = heads // n_seq
+
+    def peer(j):
+        place = 0
+        bit = 1
+        while bit < n_seq:
+            place = place + lax.rem(lax.div(seq, bit) + (j // bit) % 2, 2) * bit
+            bit *= 2
+        return place
+
+    def swap_copy(it, j, c):
+        return remote(
+            stage.at[it, j, c], kv.at[it, c, :, seq], kv_send.at[it, j, c], kv_recv.at[it, j, c], {"seq": peer(j)}
+        )
+
+    def back_copy(it, i):
+        cols = pl.ds(pl.multiple_of(seq * share * HEAD_SIZE, HEAD_SIZE), share * HEAD_SIZE)
+        return remote(piece.at[it, i], att.at[it, :, cols], o_send.at[it, i], o_recv.at[it, seq], {"seq": i})
+
+    def back_arrival(it, i):
+        cols = slice(i * share * HEAD_SIZE, (i + 1) * share * HEAD_SIZE)
+        return remote(piece.at[it, i], att.at[it, :, cols], o_send.at[it, i], o_recv.at[it, i], {"seq": i})
+
+    def exchange(it, rotated, row_scale):
+        def shaped(c, cols):
+            return (acc[c, :, cols] * row_scale).astype(bf16) if c == 2 else rotated(c, cols)
+
+        for c in (2, 1, 0):
+            for j in reversed(range(1, n_seq)):
+                for g in range(share):
+                    cols = pl.ds(pl.multiple_of((peer(j) * share + g) * HEAD_SIZE, HEAD_SIZE), HEAD_SIZE)
+                    stage[it, j, c, g] = shaped(c, cols)
+                swap_copy(it, j, c).start()
+        for c in (2, 1, 0):
+            for g in range(share):
+                cols = pl.ds(pl.multiple_of((seq * share + g) * HEAD_SIZE, HEAD_SIZE), HEAD_SIZE)
+                kv[it, c, g, seq] = shaped(c, cols)
+        for c in (2, 1, 0):
+            for j in reversed(range(1, n_seq)):
+                swap_copy(it, j, c).wait_recv()
+        for i in range(n_seq):
+            count = (i + 1) * length
+            query_index = i * length + lax.broadcasted_iota(jnp.int32, (length, count), 0)
+            allowed = lax.broadcasted_iota(jnp.int32, (length, count), 1) <= query_index
+            for g in range(share):
+                keys = kv[it, 1, g, :i + 1].reshape(count, HEAD_SIZE)
+                values = kv[it, 2, g, :i + 1].reshape(count, HEAD_SIZE)
+                scores = lax.dot_general(
+                    kv[it, 0, g, i], keys, (((1,), (1,)), ((), ())), preferred_element_type=f32
+                ) * HEAD_SIZE ** (-0.5)
+                scores = jnp.where(allowed, scores, -1e30)
+                weights = jnp.where(allowed, jnp.exp(scores - jnp.max(scores, axis=1, keepdims=True)), 0.0)
+                total = jnp.sum(weights, axis=1, keepdims=True)
+                mixture = jnp.dot(weights.astype(bf16), values, preferred_element_type=f32)
+                piece[it, i, :, g * HEAD_SIZE:(g + 1) * HEAD_SIZE] = (mixture / total).astype(bf16)
+
+            @pl.when(seq == i)
+            def _():
+                att[it, :, i * share * HEAD_SIZE:(i + 1) * share * HEAD_SIZE] = piece[it, i]
+
+            guarded(seq != i, back_copy(it, i).start)
+        for i in range(n_seq):
+            guarded(seq != i, back_arrival(it, i).wait_recv)
+
     for it in range(ITERS):
         last = it + 1 == ITERS
-        alpha = [a[:, :1] for a in anderson_weights(gram)]
-
-        def mix_step(i, carry):
+        alpha = anderson_weights(gram)
+        groups = width // LANES
+
+        def mix_step(i, sums):
             rows = pl.ds(pl.multiple_of(i * CH, CH), CH)
-            stored = [images[m, rows, :] for m in range(it, mem)] + ([image_out[rows, :]] if it else [])
-            mixed = alpha[0] * stored[0]
-            for m in range(1, mem):
-                mixed = mixed + alpha[m] * stored[m]
-            mixed_out[rows, :] = mixed
-            ready = (mixed * gain_in[...]).astype(bf16)
-            for q in range(halves):
-                xbuf[it, tp, q, rows, :] = ready[:, q * part:(q + 1) * part]
-            colbuf[rows, :] = jnp.broadcast_to(jnp.sum(mixed * mixed, axis=1, keepdims=True), (CH, 128))
-            return carry
-
-        lax.fori_loop(0, chunks, mix_step, 0)
+            squares = None
+            sums = list(sums)
+            for c in range(groups):
+                cols = slice(c * LANES, (c + 1) * LANES)
+                stored = [images[m, rows, cols] for m in range(it, mem)] + ([image_out[rows, cols]] if it else [])
+                mixed = alpha[0] * stored[0]
+                for m in range(1, mem):
+                    mixed = mixed + alpha[m] * stored[m]
+                mixed_out[rows, cols] = mixed
+                ready = (mixed * gain_in[:, cols]).astype(bf16)
+                xbuf[it, tp, c * LANES // part, rows, c * LANES % part:c * LANES % part + LANES] = ready
+                square = mixed * mixed
+                squares = square if squares is None else squares + square
+                if not last:
+                    for m in range(1, mem):
+                        sums[m - 1] = sums[m - 1] + mixed * (images[m, rows, cols] - iterates[m, rows, cols])
+            if not last:
+                sums[mem - 1] = sums[mem - 1] + squares
+            colbuf[rows, :] = squares
+            return tuple(sums)
+
+        fixed = lax.fori_loop(
+            0, chunks, mix_step, () if last else tuple(jnp.zeros((CH, LANES), f32) for _ in range(mem))
+        )
 
         def x_copy(side, k, q):
             slot = (z - steps[side] * (k - 1)) * 2 + core
@@ -228,8 +314,10 @@
                 guarded(inside(z + steps[side]), x_copy(side, 1, q).start)
         for q in range(halves):
             relay(0, 0, q).start()
-        tp_stat[1 + 2 * it, tp] = jnp.transpose(colbuf[...])[:16, :]
-        square_copies = post_tp(1 + 2 * it, 1)
+        tp_stat[1 + 2 * it, tp, :1] = jnp.sum(jnp.transpose(colbuf[...]), axis=0, keepdims=True)
+        if not last:
+            tp_stat[1 + 2 * it, tp, 1:2] = packed(fixed)
+        square_copies = post_tp(1 + 2 * it, 1 if last else 2)
         if it == 0:
             loads[0].wait()
         acc[...] = jnp.zeros(acc.shape, f32)
@@ -260,7 +348,10 @@
                     )
                 for side in range(2):
                     guarded(inside(z - steps[side] * k), functools.partial(across, side, k, q))
-        squares = collect(tp_stat, square_copies, 1 + 2 * it, n_tp, 1)
+        squares = collect(tp_stat, square_copies, 1 + 2 * it, n_tp, 1 if last else 2)
+        if not last:
+            fixed = unpacked(squares[1:2, :]) * (1.0 / LANES)
+            squares = squares[:1, :]
         row_scale = jnp.transpose(
             jnp.broadcast_to(lax.rsqrt(squares / full_width + epsilon), (length, length))
         )
@@ -273,7 +364,9 @@
             return (rows * cosine + pltpu.roll(rows, HEAD_SIZE // 2, 1) * sine).astype(bf16)
 
         kv_copies = [[] for _ in range(heads)]
-        for h in range(heads):
+        if swap:
+            exchange(it, rotated, row_scale)
+        for h in range(0 if swap else heads):
             cols = slice(h * HEAD_SIZE, (h + 1) * HEAD_SIZE)
             kv[it, h, seq, 0] = rotated(1, cols)
             kv[it, h, seq, 1] = (acc[2, :, cols] * row_scale).astype(bf16)
@@ -284,14 +377,14 @@
                 )
                 guarded(seq + d < n_seq, copy.start)
                 kv_copies[h].append((d, copy))
-        for h in range(heads):
+        for h in range(0 if swap else heads):
             cols = slice(h * HEAD_SIZE, (h + 1) * HEAD_SIZE)
             qbuf[:, cols] = rotated(0, cols)
 
         total_keys = n_seq * length
         query_index = seq * length + lax.broadcasted_iota(jnp.int32, (length, total_keys), 0)
         allowed = lax.broadcasted_iota(jnp.int32, (length, total_keys), 1) <= query_index
-        for h in range(heads):
+        for h in range(0 if swap else heads):
             cols = slice(h * HEAD_SIZE, (h + 1) * HEAD_SIZE)
             for d, copy in kv_copies[h]:
                 guarded(seq >= d, copy.wait_recv)
@@ -304,14 +397,14 @@
             weights = jnp.where(allowed, jnp.exp(scores - jnp.max(scores, axis=1, keepdims=True)), 0.0)
             total = jnp.sum(weights, axis=1, keepdims=True)
             mixture = jnp.dot(weights.astype(bf16), values, preferred_element_type=f32)
-            att[:, cols] = (mixture / total).astype(bf16)
+            att[it, :, cols] = (mixture / total).astype(bf16)
 
         if it == 0:
             loads[1].wait()
 
         def partial(place, side_core, q):
             cols = pl.ds(pl.multiple_of((place * 2 + side_core) * width + q * part, 128), part)
-            return jnp.dot(att[...], out_w[:, cols], preferred_element_type=f32)
+            return jnp.dot(att[it], out_w[:, cols], preferred_element_type=f32)
 
         def p_copy(side, k, q):
             return remote(
@@ -348,16 +441,26 @@
             zsend[it, side, k, q] = own.astype(bf16)
             z_copy(side, k, q).start()
 
-        for k in reversed(range(1, n_z)):
-            for q in range(halves):
+        order = [(k, q) for k in reversed(range(1, n_z)) for q in range(halves)]
+        offers = order + [(0, q) for q in range(halves)]
+        ahead = 2 * halves
+
+        def offer(k, q):
+            if k == 0:
+                give(0, 0, q)
+            else:
                 for side in range(2):
                     guarded(inside(z + steps[side] * k), functools.partial(give, side, k, q))
-        for q in range(halves):
-            give(0, 0, q)
-        for k in reversed(range(1, n_z)):
-            for q in range(halves):
-                for side in range(2):
-                    guarded(inside(z + steps[side] * k), functools.partial(pass_on, side, k, q))
+
+        for k, q in offers[:ahead]:
+            offer(k, q)
+        for i, (k, q) in enumerate(order):
+            for side in range(2):
+                guarded(inside(z + steps[side] * k), functools.partial(pass_on, side, k, q))
+            if ahead + i < len(offers):
+                offer(*offers[ahead + i])
+        for k, q in offers[ahead + len(order):]:
+            offer(k, q)
         for q in range(halves):
             cols = slice(q * part, (q + 1) * part)
             own = partial(z, core, q) + tokens[:, cols].astype(f32)
@@ -379,10 +482,8 @@
             summed[rows, :] = scaled
             stats = [layer * layer]
             if not last:
-                mixed = mixed_out[rows, :]
-                kept = [images[m, rows, :] - iterates[m, rows, :] for m in range(1, mem)]
-                stats += [scaled * k for k in kept] + [mixed * k for k in kept]
-                stats += [scaled * scaled, scaled * mixed, mixed * mixed]
+                stats += [scaled * (images[m, rows, :] - iterates[m, rows, :]) for m in range(1, mem)]
+                stats += [scaled * scaled, scaled * mixed_out[rows, :]]
             columns = jnp.zeros((CH, 128), f32)
             for k, stat in enumerate(stats):
                 columns = jnp.where(lane == k, jnp.sum(stat, axis=1, keepdims=True), columns)
@@ -390,31 +491,26 @@
             return carry
 
         lax.fori_loop(0, chunks, sum_step, 0)
-        tp_stat[2 + 2 * it, tp] = jnp.transpose(colbuf[...])[:16, :]
-        count = 1 if last else 16
+        count = 1 if last else mem + 2
+        tp_stat[2 + 2 * it, tp, :count] = jnp.transpose(colbuf[...])[:count, :]
         stats = collect(tp_stat, post_tp(2 + 2 * it, count), 2 + 2 * it, n_tp, count)
         scale_row = lax.rsqrt(stats[:1, :] / full_width + epsilon)
 
         if not last:
-            k = mem - 1
-            for m in range(k):
-                seq_stat[1, seq, pl.ds(m, 1), :] = (
-                    scale_row * stats[1 + m:2 + m, :] - stats[1 + k + m:2 + k + m, :]
-                )
-            own = 1 + 2 * k
-            seq_stat[1, seq, pl.ds(k, 1), :] = (
-                scale_row * scale_row * stats[own:own + 1, :]
-                - 2.0 * scale_row * stats[own + 1:own + 2, :]
-                + stats[own + 2:own + 3, :]
-            )
-            seq_stat[1, seq, pl.ds(mem, 16 - mem), :] = jnp.zeros((16 - mem, 128), f32)
-            seq_copies = post_seq(1)
+            seq_stat[1, seq, :mem - 1] = scale_row * stats[1:mem, :] - fixed[:mem - 1, :]
+            seq_stat[1, seq, mem - 1:mem] = (
+                scale_row * scale_row * stats[mem:mem + 1, :]
+                - 2.0 * scale_row * stats[mem + 1:mem + 2, :]
+                + fixed[mem - 1:mem, :]
+            )
+            seq_copies = post_seq(1, mem)
         scale_cols = jnp.transpose(jnp.broadcast_to(scale_row, (length, length)))
         for c in range(width // 128):
             cols = slice(c * 128, (c + 1) * 128)
             image_out[:, cols] = summed[:, cols] * scale_cols
         if not last:
-            new = spread(collect(seq_stat, seq_copies, 1, n_seq))
+            new = collect(seq_stat, seq_copies, 1, n_seq, mem)
+            new = jnp.broadcast_to(jnp.sum(new, axis=1, keepdims=True), new.shape)
             grown = [[None] * mem for _ in range(mem)]
             for m in range(mem - 1):
                 for n in range(mem - 1):
@@ -426,6 +522,12 @@
         for h in range(heads):
             for d, copy in kv_copies[h]:
                 guarded(seq + d < n_seq, copy.wait_send)
+        if swap:
+            for j in range(1, n_seq):
+                for c in range(3):
+                    swap_copy(it, j, c).wait_send()
+            for i in range(n_seq):
+                guarded(seq != i, back_copy(it, i).wait_send)
         for q in range(halves):
             relay(0, 0, q).wait_send()
             p_copy(0, 0, q).wait_send()
@@ -454,6 +556,19 @@
         heads = embed // HEAD_SIZE
         halves = 2 if width % 256 == 0 else 1
         part = width // halves
+        swap = swaps_heads(n_seq, heads)
+        share = max(heads // n_seq, 1)
+        if swap:
+            kv_shape = (ITERS, 3, share, n_seq, length, HEAD_SIZE)
+            kv_sems = (ITERS, n_seq, 3)
+            stage_shape = (ITERS, n_seq, 3, share, length, HEAD_SIZE)
+            piece_shape = (ITERS, n_seq, length, share * HEAD_SIZE)
+            query_shape = (8, 128)
+        else:
+            kv_shape = (ITERS, heads, n_seq, 2, length, HEAD_SIZE)
+            kv_sems = (ITERS, heads, n_seq)
+            stage_shape = piece_shape = (8, 128)
+            query_shape = (length, embed)
         vmem = pl.BlockSpec(memory_space=pltpu.VMEM)
         hbm = pl.BlockSpec(memory_space=pl.ANY)
         dma = pltpu.SemaphoreType.DMA
@@ -469,25 +584,28 @@
                 pltpu.VMEM((2, length, HEAD_SIZE), f32),
                 pltpu.VMEM((ITERS, n_tp, halves, length, part), bf16),
                 pltpu.VMEM((3, length, embed), f32),
-                pltpu.VMEM((ITERS, heads, n_seq, 2, length, HEAD_SIZE), bf16),
-                pltpu.VMEM((length, embed), bf16),
-                pltpu.VMEM((length, embed), bf16),
+                pltpu.VMEM(kv_shape, bf16),
+                pltpu.VMEM(query_shape, bf16),
+                pltpu.VMEM((ITERS, length, embed), bf16),
                 pltpu.VMEM((ITERS, 2, n_z, halves, length, part), bf16),
                 pltpu.VMEM((ITERS, 2, n_z, halves, length, part), bf16),
                 pltpu.VMEM((ITERS, 2, n_z, halves, length, part), bf16),
                 pltpu.VMEM((ITERS, 2, n_z, halves, length, part), bf16),
                 pltpu.VMEM((length, width), f32),
                 pltpu.VMEM((length, 128), f32),
-                pltpu.VMEM((1 + 2 * ITERS, n_tp, 16, 128), f32),
-                pltpu.VMEM((ITERS, n_seq, 16, 128), f32),
+                pltpu.VMEM((1 + 2 * ITERS, n_tp, 8, 128), f32),
+                pltpu.VMEM((ITERS, n_seq, 8, 128), f32),
+                pltpu.VMEM(stage_shape, bf16),
+                pltpu.VMEM(piece_shape, bf16),
                 dma((3,)),
                 dma((1 + 2 * ITERS, n_tp)), dma((1 + 2 * ITERS, n_tp)),
                 dma((ITERS, n_seq)), dma((ITERS, n_seq)),
                 dma((ITERS, 2, n_z, halves)), dma((ITERS, 2, n_z, halves)),
                 dma((ITERS, 2, n_z, halves)), dma((ITERS, 2, n_z, halves)),
-                dma((ITERS, heads, n_seq)), dma((ITERS, heads, n_seq)),
+                dma(kv_sems), dma(kv_sems),
                 dma((ITERS, 2, n_z, halves)), dma((ITERS, 2, n_z, halves)),
                 dma((ITERS, 2, n_z, halves)), dma((ITERS, 2, n_z, halves)),
+                dma((ITERS, n_seq)), dma((ITERS, n_seq)),
             ],
             compiler_params=pltpu.CompilerParams(
                 collective_id=0, has_side_effects=True, vmem_limit_bytes=60 * 1024 * 1024

time: 117 us -> 109 us (0.932)
  the two profiles are of different devices: /device:TPU:2 before, /device:TPU:0 now
where the time goes in v1:
time: 109 us
  Pallas kernels  105 us (96%)
  local copies, waits for them, and re-layouts  3.34 us (3%)
    pallas_call x1, Pallas kernels, shards(): pl.pallas_call(functools.partial(kernel, n_seq, n_tp), out_shape=(out, ou...  105 us
    unnamed x2, local copies, waits for them, and re-layouts  3.34 us

profile of v1, /device:TPU:0, one launch (start us, length us, event | category | flops | bytes accessed | tf_op | source)
XLA Modules:
  0.0 108.6 jit_solution(18248348262918643323)
XLA Ops:
  0.6 104.6 %anderson_layer.1 = (f32[128,512]{1,0:T(8,128)}, f32[128,512]{1,0:T(8,128)}) custom-call(bf16[128,512]{1,0:T(8,128)(2,1)} %bitcast.13, bf16[3,4096,512]{2,1,0:T(8,128)(2,1)} %bitcast.8, bf16[512,4096]{1,0:T(8,128)(2,1)} %out_hbm.1, f32[1,512]{1,0:T(1,128)} %bitcast.14, f32[1,512]{1,0:T(1,128)} %bitcast.15, f32[5,128,512]{2,1,0:T(8,128)} %bitcast.9, ...), custom_call_target="tpu_custom_call" | custom-call | tf_op jit(solution)/shard_map/anderson_layer/pallas_call | solution.py:576
  105.2 1.7 %copy.12 = f32[1,128,512]{2,1,0:T(8,128)} copy(f32[1,128,512]{2,1,0:T(8,128)} %bitcast.12) | data formatting | bytes 524288
  106.9 1.7 %copy.13 = f32[1,128,512]{2,1,0:T(8,128)} copy(f32[1,128,512]{2,1,0:T(8,128)} %bitcast.11) | data formatting | bytes 524288
